TPU v7x, 256 devices: a whole 4x4x8 slice. The times are simulated.
256 devices in a mesh: dom: 256 (over y, z, x, core).
Axes of the slice: x: 4, y: 4, z: 8, core: 2. Of those that a mesh axis runs over, the one named last changes fastest.
Arguments:
- particles: bfloat16 [8192, 2, 7488], P('dom'), may hold values from -6 to 6
- references: bfloat16 [256, 2, 7488], P('dom'), may hold values from -6 to 6
- assignment: int32 [8192, 1], P('dom'), may hold values from 0 to 255
- orientation: int32 [8192], P('dom'), may hold values from 0 to 35
- tilt_range: int32 [2, 8192], P(None, 'dom'), may hold values from 0 to 20
Outputs:
- scores: float32 [8192, 256], P('dom')
- class_means: float32 [256, 2, 7488], P('dom')
- class_load: float32 [256], replicated
Inputs may be any that keep to these rules, and one draw needn't show every extreme that they name: `assignment`: every class has at least one particle.
All inputs are finite; a program needn't handle non-finite values.
Results may differ from a plain program's by a relative error of at most 0.0035.
Values may be sent and summed in bfloat16 or wider, within the bound.
A program may use at most 128 MiB of HBM per device.

v0:
```python
import math
import jax
import jax.numpy as jnp
from jax import lax
from jax.sharding import Mesh
from jax.sharding import PartitionSpec as P

GRID = 24
ORIENTS = 36
COEF = 7488
DOM = ("dom_0", "dom_1", "dom_2", "dom_3")
EPS = 1e-06
GAIN = 6.0
TAU = 0.5
member_rows = 256


def cut_along(shard, dim, size):
    before, after = (shard.shape[:dim], shard.shape[dim + 1 :])
    return jnp.moveaxis(shard.reshape(*before, size, -1, *after), dim, 0)


def summed_on_arrival(shard, axis, dim):
    tiles = cut_along(shard, dim, lax.axis_size(axis))
    arrived = lax.all_to_all(tiles, axis, split_axis=0, concat_axis=0, tiled=True)
    return arrived.astype(jnp.float32).sum(axis=0)


def sum_in_two_steps(shard, axes, dim):
    far, near = axes
    own = summed_on_arrival(cut_along(shard, dim, lax.axis_size(far)), near, dim + 1)
    return jnp.sum(
        lax.all_to_all(own.astype(jnp.bfloat16), far, 0, 0, tiled=True).astype(jnp.float32), axis=0
    )


def tables():
    index = jnp.arange(COEF, dtype=jnp.int32)
    plane = index // (GRID * GRID)
    rest = index % (GRID * GRID)
    col_x = rest // GRID
    col_z = rest % GRID
    freq_x = ((col_x + GRID // 2) % GRID - GRID // 2).astype(jnp.float32)
    freq_y = plane.astype(jnp.float32)
    freq_z = ((col_z + GRID // 2) % GRID - GRID // 2).astype(jnp.float32)
    return (freq_x, freq_y, freq_z)


def wedge_weights(orient, low_bin, high_bin):
    freq_x, freq_y, freq_z = tables()
    angle = orient.astype(jnp.float32) * (2.0 * math.pi / ORIENTS)
    along = -freq_x[None, :] * jnp.sin(angle)[:, None] + freq_y[None, :] * jnp.cos(angle)[:, None]
    radius = along * along + freq_z[None, :] * freq_z[None, :] + 1.0
    cos_two = (along * along - freq_z[None, :] * freq_z[None, :]) / radius
    sin_two = -2.0 * along * freq_z[None, :] / radius
    low = -(40.0 + 1.5 * low_bin.astype(jnp.float32)) * (math.pi / 180.0)
    high = (40.0 + 1.5 * high_bin.astype(jnp.float32)) * (math.pi / 180.0)
    centre = (low + high)[:, None]
    width = (high - low)[:, None]
    return jax.nn.sigmoid(
        GAIN * (cos_two * jnp.cos(centre) + sin_two * jnp.sin(centre) - jnp.cos(width))
    )


def body(particles, references, assignment, orientation, tilt_range):
    part_rows = particles.shape[0]
    coef = particles.shape[2]
    owned = references.shape[0]
    devices = lax.axis_size(DOM)
    classes = owned * devices
    total = part_rows * devices
    cls = assignment[:, 0]
    wedge = wedge_weights(orientation, tilt_range[0], tilt_range[1])
    pf = particles.astype(jnp.float32)
    weighted = (wedge[:, None, :] * pf).astype(jnp.bfloat16)
    flat = weighted.reshape(part_rows, 2 * coef)
    wedge_low = wedge.astype(jnp.bfloat16)
    power = jnp.sum(wedge * (pf[:, 0] * pf[:, 0] + pf[:, 1] * pf[:, 1]), axis=1)
    piece = lax.all_gather(references, DOM, axis=0, tiled=True)
    count = piece.shape[0]
    p32 = piece.astype(jnp.float32)
    ref_power = (p32[:, 0] * p32[:, 0] + p32[:, 1] * p32[:, 1]).astype(jnp.bfloat16)
    intersection = lax.dot_general(
        flat,
        piece.reshape(count, 2 * coef),
        (((1,), (1,)), ((), ())),
        preferred_element_type=jnp.float32,
    )
    energy = lax.dot_general(
        wedge_low, ref_power, (((1,), (1,)), ((), ())), preferred_element_type=jnp.float32
    )
    scores = intersection / (
        math.sqrt(coef) * jnp.sqrt((energy / coef + EPS) * (power[:, None] / coef + EPS))
    )
    ids = lax.iota(jnp.int32, owned * lax.axis_size(DOM))
    onehot = (ids[:, None] == cls[None, :]).astype(jnp.bfloat16)
    numer = sum_in_two_steps(
        jnp.dot(onehot, flat, preferred_element_type=jnp.float32).astype(jnp.bfloat16),
        (("dom_0", "dom_1"), ("dom_2", "dom_3")),
        0,
    )
    labels = jnp.stack([cls, orientation, tilt_range[0], tilt_range[1]])
    every = lax.all_gather(labels, DOM, axis=1, tiled=True)
    class_ids = jnp.arange(classes, dtype=jnp.int32)
    counts = jnp.sum((class_ids[:, None] == every[0][None, :]).astype(jnp.float32), axis=1)
    own_class = lax.axis_index(DOM) * owned + 0
    chosen = every[0] == own_class
    members = jnp.nonzero(chosen, size=total + member_rows, fill_value=0)[0].astype(jnp.int32)
    members_count = jnp.sum(chosen.astype(jnp.int32))
    block_count = (members_count + member_rows - 1) // member_rows

    def member_block(block, acc):
        square_sum, wedge_sum = acc
        first = (block * member_rows).astype(jnp.int32)
        picked = lax.dynamic_slice_in_dim(members, first, member_rows, 0)
        valid = (first + lax.iota(jnp.int32, member_rows) < members_count).astype(jnp.float32)
        member_wedge = wedge_weights(every[1][picked], every[2][picked], every[3][picked])
        squares = (member_wedge * member_wedge).astype(jnp.bfloat16).astype(jnp.float32)
        square_sum = square_sum + jnp.sum(valid[:, None] * squares, axis=0)
        wedge_sum = wedge_sum + jnp.sum(valid * jnp.sum(member_wedge, axis=1))
        return (square_sum, wedge_sum)

    square_sum, wedge_sum = lax.fori_loop(
        0, block_count, member_block, (jnp.zeros((coef,), jnp.float32), jnp.zeros((), jnp.float32))
    )
    denom_rows = [square_sum]
    total_rows = [wedge_sum]
    denom = jnp.stack(denom_rows)
    own_totals = jnp.stack(total_rows)
    bottom = denom + TAU * (own_totals[:, None] / coef + 1.0)
    class_means = numer.reshape(owned, 2, coef) / bottom[:, None, :]
    class_load = counts * classes / total
    return (scores, class_means, class_load)


def solution(mesh):
    split = Mesh(mesh.devices.reshape(4, 8, 4, 2), ("dom_0", "dom_1", "dom_2", "dom_3"))
    placed = (P(DOM, None, None), P(DOM, None, None), P(DOM, None), P(DOM), P(None, DOM))
    return jax.shard_map(
        body,
        mesh=split,
        in_specs=placed,
        out_specs=(P(DOM, None), P(DOM, None, None), P()),
        check_vma=False,
    )
```

profile of v0, /device:TPU:32, one launch (start us, length us, event | category | flops | bytes accessed | tf_op | source)
XLA Modules:
  0.0 332.5 jit_solution(10021585373992793412)
XLA Ops:
  8.9 1.3 copy_convert_fusion
  11.3 1.4 multiply_convert_fusion.1
  14.1 2.1 fusion.26
  16.3 3.8 %copy.40 = bf16[32,8,1,14976]{3,0,2,1:T(8,128)(2,1)} copy(bf16[32,8,1,14976]{3,1,0,2:T(8,128)(2,1)S(1)} %fusion.26) | data formatting | bytes 15335424 | tf_op jit(solution)/shard_map/reshape;reshape | solution.py:20
  20.1 5.1 %all-to-all-start = ((bf16[8,32,1,14976]{3,1,2,0:T(8,128)(2,1)}), bf16[8,32,1,14976]{3,1,2,0:T(8,128)(2,1)}, u32[]{:S(2)}, u32[]{:S(2)}) async-start(bf16[8,32,1,14976]{3,1,2,0:T(8,128)(2,1)} %bitcast.71), calls=%async_computation | async-start | bytes 15335424 | tf_op jit(solution)/shard_map/all_to_all | solution.py:25
  25.9 150.9 %all-gather = s32[256,32,4]{1,2,0:T(4,128)S(1)} all-gather(s32[1,32,4]{1,2,0:T(4,128)S(1)} %add_bitcast_fusion), channel_id=1, replica_groups=mesh['dom_0'=4,'dom_1'=8,'dom_2'=4,'dom_3'=2] {'dom_0','dom_1','dom_2','..., dimensions={0}, use_global_device_ids=true | all-gather | bytes 131584 | tf_op jit(solution)/shard_map/all_gather | solution.py:103
  179.3 57.2 %scatter_custom_fusion = s32[8448]{0:T(1024)S(1)} fusion(s32[8192]{0:T(1024)S(1)} %bitcast.81, s32[8192]{0:T(1024)S(1)} %broadcast.1000, s32[]{:T(128)} %constant.270.clone.1), kind=kCustom, calls=%fused_computation.125 | custom fusion | flops 8192 | bytes 33796 | tf_op jit(solution)/shard_map/scatter-add | solution.py:108
  237.8 4.4 %reduce_sum.94 = bf16[32,14976]{1,0:T(8,128)(2,1)S(1)} reduce(bf16[8,32,1,14976]{3,1,2,0:T(8,128)(2,1)} %all-to-all-done, bf16[]{:T(256)} %constant.286.clone.1), dimensions={0,2}, to_apply=%region_1.2 | reduce | flops 3354624 | bytes 8626178 | tf_op jit(solution)/shard_map/reduce_sum | solution.py:26
  242.7 1.4 reduce.7
  244.1 2.0 reshape.541
  246.1 7.1 %all-to-all-start.1 = ((bf16[32,2,7488]{2,1,0:T(2,128)(2,1)}), bf16[32,2,7488]{2,1,0:T(2,128)(2,1)}, u32[]{:S(2)}, u32[]{:S(2)}) async-start(bf16[32,2,7488]{2,1,0:T(2,128)(2,1)} %reshape.541), calls=%async_computation.1 | async-start | bytes 1933312 | tf_op jit(solution)/shard_map/all_to_all | solution.py:33
  253.2 15.0 %while.15 = (s32[]{:T(128)}, f32[7488]{0:T(1024)S(1)}, f32[]{:T(128)}, s32[]{:T(128)}, s32[]{:T(128)}, /*index=5*/s32[4,8192]{1,0:T(4,128)S(1)}, s32[8448]{0:T(1...) while((s32[]{:T(128)}, f32[7488]{0:T(1024)S(1)}, f32[]{:T(128)}, s32[]{:T(128)}, s32[]{:T(128)}, ...), condition=%wide.region_13.14_spmd, body=%wide.region_9.13_spmd.sunk | while | flops 46529604 | bytes 592063 | solution.py:123
  254.3 1.7 gather_fusion
  256.0 1.7 gather_fusion.1
  257.7 1.7 gather_fusion.2
  259.6 6.5 %fusion.100 = (f32[256]{0:T(256)S(1)}, f32[7488]{0:T(1024)S(1)}) fusion(f32[256]{0:T(256)S(1)} %get-tuple-element.240, f32[256]{0:T(256)S(1)} %sin.43, f32[7488]{0:T(1024)S(1)} %get-tuple-element.242, f32[256]{0:T(256)S(1)} %get-tuple-element.243, f32[7488]{0:T(1024)S(1)} %fusion.97, f32[256]{0:T(256)S(1)} %get-tuple-element.244, ...), kind=kLoop, calls=%fused_computation.7.clone.1 | loop fusion | flops 45998528 | bytes 156928 | tf_op jit(solution)/shard_map/while/body/reduce_sum | solution.py:120
  266.1 1.2 select_reduce_fusion.2
  270.0 10.2 %all-to-all-done.1 = bf16[32,2,7488]{2,1,0:T(2,128)(2,1)} async-done(((bf16[32,2,7488]{2,1,0:T(2,128)(2,1)}), bf16[32,2,7488]{2,1,0:T(2,128)(2,1)}, u32[]{:S(2)}, u32[]{:S(2)}) %all-to-all-start.1) | async-done | bytes 958496 | tf_op jit(solution)/shard_map/all_to_all | solution.py:33
  280.2 4.5 %reshape.542 = bf16[32,1,14976]{2,1,0:T(2,128)(2,1)S(1)} reshape(bf16[32,2,7488]{2,1,0:T(2,128)(2,1)} %all-to-all-done.1) | data formatting | bytes 1916928
  284.7 2.0 convert_reduce_fusion.1
  287.5 19.6 %copy.31 = bf16[256,2,7488]{0,2,1:T(8,128)(2,1)} copy(bf16[256,2,7488]{2,1,0:T(2,128)(2,1)} %all-gather.3.cloned.1.call-done) | data formatting | bytes 15335424 | tf_op jit(solution)/shard_map/all_gather | solution.py:79
  307.0 9.9 %convert_element_type.241 = f32[256,2,7488]{0,2,1:T(8,128)} convert(bf16[256,2,7488]{0,2,1:T(8,128)(2,1)} %copy.31) | non-fusion elementwise | flops 3833856 | bytes 23003136 | tf_op jit(solution)/shard_map/convert_element_type | solution.py:81
  317.0 6.5 %fusion.45 = f32[32,256]{1,0:T(8,128)S(1)} fusion(f32[256,2,7488]{0,2,1:T(8,128)} %convert_element_type.241, f32[32]{0:T(128)S(1)} %multiply_add_fusion, f32[32]{0:T(128)S(1)} %get-tuple-element.176, f32[32]{0:T(128)S(1)} %get-tuple-element.175, f32[7488]{0:T(1024)S(1)} %get-tuple-element.180, f32[32]{0:T(128)S(1)} %get-tuple-element.174, ...), kind=kOutput, calls=%fused_computation.71 | convolution fusion | flops 134936576 | bytes 15488768 | tf_op jit(solution)/shard_map/dot_general | solution.py:89
  323.6 2.0 fusion.32
  (59 shorter events, 12.2 us)
Async XLA Ops:
  7.2 7.0 %copy-start = (s32[32,1]{0,1:T(1,128)S(1)}, s32[32,1]{0,1:T(1,128)}, u32[]{:S(2)}) copy-start(s32[32,1]{0,1:T(1,128)} %param.9) | copy-start | bytes 388
  20.1 5.8 %copy-start.1 = (s32[2,32]{1,0:T(2,128)S(1)}, s32[2,32]{1,0:T(2,128)}, u32[]{:S(2)}) copy-start(s32[2,32]{1,0:T(2,128)} %param.11) | copy-start | bytes 772
  20.1 5.8 %copy-start.2 = (s32[32]{0:T(128)S(1)}, s32[32]{0:T(128)}, u32[]{:S(2)}) copy-start(s32[32]{0:T(128)} %param.10) | copy-start | bytes 388
  20.1 217.7 %all-to-all-start = ((bf16[8,32,1,14976]{3,1,2,0:T(8,128)(2,1)}), bf16[8,32,1,14976]{3,1,2,0:T(8,128)(2,1)}, u32[]{:S(2)}, u32[]{:S(2)}) async-start(bf16[8,32,1,14976]{3,1,2,0:T(8,128)(2,1)} %bitcast.71), calls=%async_computation | async-start | bytes 15335424 | tf_op jit(solution)/shard_map/all_to_all | solution.py:25
  25.2 262.3 %all-gather.3.cloned.1.call-start = ((), (), s32[]{:S(2)}) async-start(), calls=%async_computation.2 | async-start | bytes 7763456 | tf_op jit(solution)/shard_map/all_gather | solution.py:79
  246.1 34.1 %all-to-all-start.1 = ((bf16[32,2,7488]{2,1,0:T(2,128)(2,1)}), bf16[32,2,7488]{2,1,0:T(2,128)(2,1)}, u32[]{:S(2)}, u32[]{:S(2)}) async-start(bf16[32,2,7488]{2,1,0:T(2,128)(2,1)} %reshape.541), calls=%async_computation.1 | async-start | bytes 1933312 | tf_op jit(solution)/shard_map/all_to_all | solution.py:33
  307.0 16.5 %slice-start = ((s8[7667712]{0:T(1024)(128)(4,1)}), s8[3473408]{0:T(1024)(128)(4,1)S(1)}, s32[]{:S(2)}) async-start(s8[7667712]{0:T(1024)(128)(4,1)} %bitcast.69), calls=%async_computation.3 | async-start | bytes 6946816
  317.0 6.6 %slice-start.1 = ((s8[7667712]{0:T(1024)(128)(4,1)}), s8[4194304]{0:T(1024)(128)(4,1)S(1)}, s32[]{:S(2)}) async-start(s8[7667712]{0:T(1024)(128)(4,1)} %bitcast.69), calls=%async_computation.4 | async-start | bytes 8388608
Sparse Core Ops, SparseCore 0:
  29.7 133.0 all-gather.2
where the time goes:
time: 334 us; the launch traced here: 332 us
  blocking collectives  151 us (45%)
  other arithmetic  93.9 us (28%)
  local copies, waits for them, and re-layouts  38 us (11%)
  between operations  15 us (4%)
  starting transfers between devices  12.2 us (4%)
  waiting for transfers between devices  10.9 us (3%)
  matrix products  10.7 us (3%)
    all_gather x1, blocking collectives, body(): every = lax.all_gather(labels, DOM, axis=1, tiled=True)  151 us
    scatter-add x1, other arithmetic, body(): jnp.nonzero(chosen, size=total + member_rows, fill_value=0)[0]  57.2 us
    all_gather x1, local copies, waits for them, and re-layouts, body(): piece = lax.all_gather(references, DOM, axis=0, tiled=True)  19.6 us
    all_to_all x1, waiting for transfers between devices, sum_in_two_steps(): lax.all_to_all(own.astype(jnp.bfloat16), far, 0, 0, tiled=True)  10.2 us
    convert_element_type x1, other arithmetic, body(): p32 = piece.astype(jnp.float32)  9.95 us
    reduce_sum x2, other arithmetic, member_block(): wedge_sum = wedge_sum + jnp.sum(valid * jnp.sum(member_wedge, axis=1))  7.76 us
    all_to_all x1, starting transfers between devices, sum_in_two_steps(): lax.all_to_all(own.astype(jnp.bfloat16), far, 0, 0, tiled=True)  7.06 us
    unnamed x13, local copies, waits for them, and re-layouts  6.88 us
  transfers between devices with their start and end apart: 3, of which 1 were waited for; matrix products, arithmetic and copies ran while one was open for 28% of the time, Pallas kernels for 0%

commit v1 on v0

--- a/solution.py
+++ b/solution.py
@@ -13,6 +13,13 @@
 GAIN = 6.0
 TAU = 0.5
 member_rows = 256
+
+
+def all_by_exchange(block, name, dim):
+    size = lax.axis_size(name)
+    shards = jnp.stack([block for _ in range(size)])
+    shards = lax.all_to_all(shards, name, split_axis=0, concat_axis=0)
+    return jnp.concatenate(shards, axis=dim)
 
 
 def cut_along(shard, dim, size):
@@ -100,7 +107,7 @@
         0,
     )
     labels = jnp.stack([cls, orientation, tilt_range[0], tilt_range[1]])
-    every = lax.all_gather(labels, DOM, axis=1, tiled=True)
+    every = all_by_exchange(labels, DOM, 1)
     class_ids = jnp.arange(classes, dtype=jnp.int32)
     counts = jnp.sum((class_ids[:, None] == every[0][None, :]).astype(jnp.float32), axis=1)
     own_class = lax.axis_index(DOM) * owned + 0

time: 334 us -> 238 us (0.71)
  blocking collectives: 151 us -> 0 us
  waiting for transfers between devices: 10.9 us -> 45.2 us
  starting transfers between devices: 12.2 us -> 29.8 us
    all_gather x1 -> x0, blocking collectives: 151 us -> none  [body(): every = lax.all_gather(labels, DOM, axis=1, tiled=True)]
    all_to_all x1, waiting for transfers between devices: 0.01 us -> 25.6 us  [summed_on_arrival(): lax.all_to_all(tiles, axis, split_axis=0, concat_axis=0, tiled=True)]
    all_to_all x0 -> x1, starting transfers between devices: none -> 14.4 us  [all_by_exchange(): shards = lax.all_to_all(shards, name, split_axis=0, concat_axis=0)]
    all_to_all x1, waiting for transfers between devices: 10.2 us -> 18.7 us  [sum_in_two_steps(): lax.all_to_all(own.astype(jnp.bfloat16), far, 0, 0, tiled=True)]
    all_to_all x1, starting transfers between devices: 7.06 us -> 10.5 us  [sum_in_two_steps(): lax.all_to_all(own.astype(jnp.bfloat16), far, 0, 0, tiled=True)]
    unnamed x13 -> x12, local copies, waits for them, and re-layouts: 6.88 us -> 7.87 us
  transfers between devices with their start and end apart: 3 -> 4, of which waited for: 1 -> 3; matrix products, arithmetic and copies ran while one was open for 28% -> 45% of each run, Pallas kernels for 0% -> 0%
where the time goes in v1:
time: 238 us; the launch traced here: 237 us
  other arithmetic  95.1 us (40%)
  waiting for transfers between devices  45.2 us (19%)
  local copies, waits for them, and re-layouts  40.1 us (17%)
  starting transfers between devices  29.8 us (13%)
  between operations  15 us (6%)
  matrix products  10.7 us (4%)
    scatter-add x1, other arithmetic, body(): jnp.nonzero(chosen, size=total + member_rows, fill_value=0)[0]  57.2 us
    all_to_all x1, waiting for transfers between devices, summed_on_arrival(): lax.all_to_all(tiles, axis, split_axis=0, concat_axis=0, tiled=True)  25.6 us
    all_gather x1, local copies, waits for them, and re-layouts, body(): piece = lax.all_gather(references, DOM, axis=0, tiled=True)  19.6 us
    all_to_all x1, waiting for transfers between devices, sum_in_two_steps(): lax.all_to_all(own.astype(jnp.bfloat16), far, 0, 0, tiled=True)  18.7 us
    all_to_all x1, starting transfers between devices, all_by_exchange(): shards = lax.all_to_all(shards, name, split_axis=0, concat_axis=0)  14.4 us
    all_to_all x1, starting transfers between devices, sum_in_two_steps(): lax.all_to_all(own.astype(jnp.bfloat16), far, 0, 0, tiled=True)  10.5 us
    convert_element_type x1, other arithmetic, body(): p32 = piece.astype(jnp.float32)  9.95 us
    unnamed x12, local copies, waits for them, and re-layouts  7.87 us
  transfers between devices with their start and end apart: 4, of which 3 were waited for; matrix products, arithmetic and copies ran while one was open for 45% of the time, Pallas kernels for 0%

profile of v1, /device:TPU:32, one launch (start us, length us, event | category | flops | bytes accessed | tf_op | source)
XLA Modules:
  0.0 236.8 jit_solution(16448128113148729882)
XLA Ops:
  9.0 14.4 %all-to-all-start.2 = ((s32[256,1,128]{2,1,0:T(1,128)}), s32[256,1,128]{2,1,0:T(1,128)S(1)}, u32[]{:S(2)}, u32[]{:S(2)}) async-start(s32[256,1,128]{2,1,0:T(1,128)} %reshape.566), calls=%async_computation.2 | async-start | bytes 262144 | tf_op jit(solution)/shard_map/all_to_all | solution.py:21
  25.1 1.3 copy_convert_fusion
  29.2 2.1 fusion.26
  31.3 3.9 %copy.38 = bf16[32,8,1,14976]{3,0,2,1:T(8,128)(2,1)} copy(bf16[32,8,1,14976]{3,1,0,2:T(8,128)(2,1)S(1)} %fusion.26) | data formatting | bytes 15335424 | tf_op jit(solution)/shard_map/reshape;reshape | solution.py:27
  35.4 4.9 %all-to-all-start = ((bf16[8,32,1,14976]{3,1,2,0:T(8,128)(2,1)}), bf16[8,32,1,14976]{3,1,2,0:T(8,128)(2,1)}, u32[]{:S(2)}, u32[]{:S(2)}) async-start(bf16[8,32,1,14976]{3,1,2,0:T(8,128)(2,1)} %bitcast.63), calls=%async_computation | async-start | bytes 15335424 | tf_op jit(solution)/shard_map/all_to_all | solution.py:32
  42.8 1.4 slice_reduce_fusion.2
  46.0 57.2 %scatter_custom_fusion = s32[8448]{0:T(1024)S(1)} fusion(s32[8192]{0:T(1024)S(1)} %bitcast.69, s32[8192]{0:T(1024)S(1)} %broadcast.1003, s32[]{:T(128)} %constant.270.clone.1), kind=kCustom, calls=%fused_computation.126 | custom fusion | flops 8192 | bytes 33796 | tf_op jit(solution)/shard_map/scatter-add | solution.py:115
  104.5 25.6 %all-to-all-done = bf16[8,32,1,14976]{3,1,2,0:T(8,128)(2,1)} async-done(((bf16[8,32,1,14976]{3,1,2,0:T(8,128)(2,1)}), bf16[8,32,1,14976]{3,1,2,0:T(8,128)(2,1)}, u32[]{:S(2)}, u32[]{:S(2)}) %all-to-all-start) | async-done | bytes 7667744 | tf_op jit(solution)/shard_map/all_to_all | solution.py:32
  130.2 4.4 %reduce_sum.94 = bf16[32,14976]{1,0:T(8,128)(2,1)S(1)} reduce(bf16[8,32,1,14976]{3,1,2,0:T(8,128)(2,1)} %all-to-all-done, bf16[]{:T(256)} %constant.286.clone.1), dimensions={0,2}, to_apply=%region_1.2 | reduce | flops 3354624 | bytes 8626178 | tf_op jit(solution)/shard_map/reduce_sum | solution.py:33
  135.1 1.4 reduce.16
  136.4 2.0 reshape.564
  138.5 10.5 %all-to-all-start.1 = ((bf16[32,2,7488]{2,1,0:T(2,128)(2,1)}), bf16[32,2,7488]{2,1,0:T(2,128)(2,1)}, u32[]{:S(2)}, u32[]{:S(2)}) async-start(bf16[32,2,7488]{2,1,0:T(2,128)(2,1)} %reshape.564), calls=%async_computation.1 | async-start | bytes 1933312 | tf_op jit(solution)/shard_map/all_to_all | solution.py:40
  149.0 15.0 %while.15 = (s32[]{:T(128)}, f32[7488]{0:T(1024)S(1)}, f32[]{:T(128)}, s32[]{:T(128)}, s32[]{:T(128)}, /*index=5*/s32[4,8192]{1,0:T(4,128)S(1)}, s32[8448]{0:T(1...) while((s32[]{:T(128)}, f32[7488]{0:T(1024)S(1)}, f32[]{:T(128)}, s32[]{:T(128)}, s32[]{:T(128)}, ...), condition=%wide.region_13.14_spmd, body=%wide.region_9.13_spmd.sunk | while | flops 46529604 | bytes 592063 | solution.py:130
  150.0 1.7 gather_fusion
  151.8 1.7 gather_fusion.1
  153.5 1.7 gather_fusion.2
  155.3 6.5 %fusion.102 = (f32[256]{0:T(256)S(1)}, f32[7488]{0:T(1024)S(1)}) fusion(f32[256]{0:T(256)S(1)} %get-tuple-element.243, f32[256]{0:T(256)S(1)} %sin.43, f32[7488]{0:T(1024)S(1)} %get-tuple-element.245, f32[256]{0:T(256)S(1)} %get-tuple-element.246, f32[7488]{0:T(1024)S(1)} %fusion.99, f32[256]{0:T(256)S(1)} %get-tuple-element.247, ...), kind=kLoop, calls=%fused_computation.7.clone.1 | loop fusion | flops 45998528 | bytes 156928 | tf_op jit(solution)/shard_map/while/body/reduce_sum | solution.py:127
  165.9 18.7 %all-to-all-done.1 = bf16[32,2,7488]{2,1,0:T(2,128)(2,1)} async-done(((bf16[32,2,7488]{2,1,0:T(2,128)(2,1)}), bf16[32,2,7488]{2,1,0:T(2,128)(2,1)}, u32[]{:S(2)}, u32[]{:S(2)}) %all-to-all-start.1) | async-done | bytes 958496 | tf_op jit(solution)/shard_map/all_to_all | solution.py:40
  184.6 4.5 %reshape.565 = bf16[32,1,14976]{2,1,0:T(2,128)(2,1)S(1)} reshape(bf16[32,2,7488]{2,1,0:T(2,128)(2,1)} %all-to-all-done.1) | data formatting | bytes 1916928
  189.1 2.0 convert_reduce_fusion.1
  191.9 19.6 %copy.29 = bf16[256,2,7488]{0,2,1:T(8,128)(2,1)} copy(bf16[256,2,7488]{2,1,0:T(2,128)(2,1)} %all-gather.2.cloned.1.call-done) | data formatting | bytes 15335424 | tf_op jit(solution)/shard_map/all_gather | solution.py:86
  211.4 9.9 %convert_element_type.242 = f32[256,2,7488]{0,2,1:T(8,128)} convert(bf16[256,2,7488]{0,2,1:T(8,128)(2,1)} %copy.29) | non-fusion elementwise | flops 3833856 | bytes 23003136 | tf_op jit(solution)/shard_map/convert_element_type | solution.py:88
  221.4 6.5 %fusion.45 = f32[32,256]{1,0:T(8,128)S(1)} fusion(f32[256,2,7488]{0,2,1:T(8,128)} %convert_element_type.242, f32[32]{0:T(128)S(1)} %multiply_add_fusion, f32[32]{0:T(128)S(1)} %get-tuple-element.179, f32[32]{0:T(128)S(1)} %get-tuple-element.178, f32[7488]{0:T(1024)S(1)} %get-tuple-element.183, f32[32]{0:T(128)S(1)} %get-tuple-element.177, ...), kind=kOutput, calls=%fused_computation.71 | convolution fusion | flops 134936576 | bytes 15488768 | tf_op jit(solution)/shard_map/dot_general | solution.py:96
  228.0 2.0 fusion.32
  (63 shorter events, 16.9 us)
Async XLA Ops:
  7.2 22.0 %copy-start.1 = (s32[32,1]{0,1:T(1,128)S(1)}, s32[32,1]{0,1:T(1,128)}, u32[]{:S(2)}) copy-start(s32[32,1]{0,1:T(1,128)} %param.9) | copy-start | bytes 388
  7.2 20.4 %copy-start = (bf16[32,2,7488]{2,1,0:T(2,128)(2,1)S(1)}, bf16[32,2,7488]{2,1,0:T(2,128)(2,1)}, u32[]{:S(2)}) copy-start(bf16[32,2,7488]{2,1,0:T(2,128)(2,1)} %param.7) | copy-start | bytes 2875396
  9.0 26.4 %all-to-all-start.2 = ((s32[256,1,128]{2,1,0:T(1,128)}), s32[256,1,128]{2,1,0:T(1,128)S(1)}, u32[]{:S(2)}, u32[]{:S(2)}) async-start(s32[256,1,128]{2,1,0:T(1,128)} %reshape.566), calls=%async_computation.2 | async-start | bytes 262144 | tf_op jit(solution)/shard_map/all_to_all | solution.py:21
  35.4 94.7 %all-to-all-start = ((bf16[8,32,1,14976]{3,1,2,0:T(8,128)(2,1)}), bf16[8,32,1,14976]{3,1,2,0:T(8,128)(2,1)}, u32[]{:S(2)}, u32[]{:S(2)}) async-start(bf16[8,32,1,14976]{3,1,2,0:T(8,128)(2,1)} %bitcast.63), calls=%async_computation | async-start | bytes 15335424 | tf_op jit(solution)/shard_map/all_to_all | solution.py:32
  40.3 151.5 %all-gather.2.cloned.1.call-start = ((), (), s32[]{:S(2)}) async-start(), calls=%async_computation.3 | async-start | bytes 7763456 | tf_op jit(solution)/shard_map/all_gather | solution.py:86
  138.5 46.1 %all-to-all-start.1 = ((bf16[32,2,7488]{2,1,0:T(2,128)(2,1)}), bf16[32,2,7488]{2,1,0:T(2,128)(2,1)}, u32[]{:S(2)}, u32[]{:S(2)}) async-start(bf16[32,2,7488]{2,1,0:T(2,128)(2,1)} %reshape.564), calls=%async_computation.1 | async-start | bytes 1933312 | tf_op jit(solution)/shard_map/all_to_all | solution.py:40
  211.4 16.5 %slice-start = ((s8[7667712]{0:T(1024)(128)(4,1)}), s8[3473408]{0:T(1024)(128)(4,1)S(1)}, s32[]{:S(2)}) async-start(s8[7667712]{0:T(1024)(128)(4,1)} %bitcast.61), calls=%async_computation.4 | async-start | bytes 6946816
  221.4 6.6 %slice-start.1 = ((s8[7667712]{0:T(1024)(128)(4,1)}), s8[4194304]{0:T(1024)(128)(4,1)S(1)}, s32[]{:S(2)}) async-start(s8[7667712]{0:T(1024)(128)(4,1)} %bitcast.61), calls=%async_computation.5 | async-start | bytes 8388608
Sparse Core Ops, SparseCore 0:
  44.9 144.2 all-gather.1
